TPU v7x, 32 devices: a whole 2x2x4 slice. The times are simulated.
32 devices in a mesh: tensor: 4 (over y, x), seq: 8 (over z, core).
Axes of the slice: x: 2, y: 2, z: 4, core: 2. Of those that a mesh axis runs over, the one named last changes fastest.
Arguments:
- key_states: bfloat16 [8, 2, 4096, 1024], P(None, None, 'seq', 'tensor'), may hold values from -6 to 6
- value_states: bfloat16 [8, 2, 4096, 1024], P(None, None, 'seq', 'tensor'), may hold values from -6 to 6
- bin_index: int32 [8, 8, 4096], P(None, 'tensor', 'seq'), may hold values from 0 to 4095
- retain_count: int32 [8], replicated, may hold values from 1 to 4096
Outputs:
- histogram: float32 [8, 8, 2, 4096], P(None, 'tensor', None, 'seq')
- threshold: int32 [8], replicated
All inputs are finite; a program needn't handle non-finite values.
Results may differ from a plain program's by a relative error of at most 0.0029.
Values sent between devices are 32-bit elements; how exact they have to be, the bound alone decides.
A program may use at most 64 MiB of HBM per device.

v0:
```python
import functools

import jax
import jax.numpy as jnp
from jax import lax
from jax.experimental import pallas as pl
from jax.experimental.pallas import tpu as pltpu
from jax.sharding import PartitionSpec as P

BINS = 4096
MESH = pl.DeviceIdType.MESH
NT = (((1,), (1,)), ((), ()))
F32 = jnp.float32
BF16 = jnp.bfloat16


def iota(shape, dim):
    return lax.broadcasted_iota(jnp.int32, shape, dim)


def each(lo, hi, body):
    if hi - lo <= 8:
        for k in range(lo, hi):
            body(k)
    else:

        @pl.loop(lo, hi)
        def _(k):
            body(k)


def exact_dot(a, b):
    return jnp.dot(a, b, precision=lax.Precision.HIGHEST, preferred_element_type=F32)


def kernel(
    n, nt, key_hbm, value_hbm, bins, retain, out, threshold,
    kbuf, vbuf, lo_hot, stage_c, recv_c, mine_t, recv_t, all_x, stage_h, recv_d, comb, recv_h,
    in_sem, cs, cr, ts, tr, gs, gr, ds, dr, hs, hr,
):
    pairs, heads, toks = bins.shape
    width = kbuf.shape[3] // heads
    lanes = stage_c.shape[2]
    his = BINS // lanes
    per = his // n
    group, chips = 2 * nt, n // 2
    per_c = his // group
    me = lax.axis_index("seq")
    my_t = lax.axis_index("tensor")
    chip, core = me // 2, me % 2
    spot = my_t * 2 + core

    def in_plane(k):
        g = lax.rem(spot + k, group)
        return g, {"seq": chip * 2 + g % 2, "tensor": g // 2}

    def in_line(k):
        z = lax.rem(chip + k, chips)
        return z, {"seq": z * 2 + core}

    def loads(p):
        return (
            pltpu.make_async_copy(key_hbm.at[p], kbuf.at[p], in_sem.at[0, p]),
            pltpu.make_async_copy(value_hbm.at[p], vbuf.at[p], in_sem.at[1, p]),
        )

    for p in range(pairs):
        for c in loads(p):
            c.start()

    barrier = pltpu.get_barrier_semaphore()

    def greet(k):
        pl.semaphore_signal(barrier, inc=1, device_id=in_plane(k)[1], device_id_type=MESH)

    def greet_line(k):
        pl.semaphore_signal(barrier, inc=1, device_id=in_line(k)[1], device_id_type=MESH)

    each(1, group, greet)
    each(1, chips, greet_line)

    shift = lanes.bit_length() - 1
    for p in range(pairs):
        count = jnp.zeros((his, lanes), F32)
        for h in range(heads):
            row = bins[p, pl.ds(h, 1), :]
            low = row & (lanes - 1)
            high = row >> shift
            lo_mat = jnp.where(iota((lanes, toks), 0) == low, 1.0, 0.0).astype(BF16)
            lo_hot[p, h] = lo_mat
            hi_mat = jnp.where(iota((his, toks), 0) == high, 1.0, 0.0).astype(BF16)
            count += lax.dot_general(hi_mat, lo_mat, NT, preferred_element_type=F32)
        for o in range(group):
            stage_c[o, pl.ds(p * per_c, per_c), :] = count[o * per_c:(o + 1) * per_c, :]

    def copy_c(k):
        g, device = in_plane(k)
        return pltpu.make_async_remote_copy(
            src_ref=stage_c.at[g], dst_ref=recv_c.at[k], send_sem=cs.at[k], recv_sem=cr.at[k],
            device_id=device, device_id_type=MESH)

    def copy_t(k):
        return pltpu.make_async_remote_copy(
            src_ref=mine_t, dst_ref=recv_t.at[k], send_sem=ts.at[k], recv_sem=tr.at[k],
            device_id=in_line(k)[1], device_id_type=MESH)

    def copy_g(k, slot):
        return pltpu.make_async_remote_copy(
            src_ref=all_x.at[slot], dst_ref=all_x.at[slot], send_sem=gs.at[k], recv_sem=gr.at[k],
            device_id=in_plane(k)[1], device_id_type=MESH)

    def copy_d(p):
        return pltpu.make_async_remote_copy(
            src_ref=stage_h.at[p, 1 - core], dst_ref=recv_d.at[p], send_sem=ds.at[p], recv_sem=dr.at[p],
            device_id={"seq": chip * 2 + 1 - core}, device_id_type=MESH)

    def copy_h(k, p):
        z, device = in_line(k)
        return pltpu.make_async_remote_copy(
            src_ref=comb.at[z, p], dst_ref=recv_h.at[k, p], send_sem=hs.at[k], recv_sem=hr.at[k],
            device_id=device, device_id_type=MESH)

    def copy_h_all(k):
        z, device = in_line(k)
        return pltpu.make_async_remote_copy(
            src_ref=comb.at[z], dst_ref=recv_h.at[k], send_sem=hs.at[k], recv_sem=hr.at[k],
            device_id=device, device_id_type=MESH)

    blk = 128
    eye = iota((blk, blk), 0) == iota((blk, blk), 1)

    def diag(g):
        return jnp.sum(jnp.where(eye, g, 0.0), axis=0, keepdims=True)

    def cosine(buf, p, h):
        parts = []
        for t in range(0, toks, blk):
            a = buf[p, 0, t:t + blk, h * width:(h + 1) * width]
            b = buf[p, 1, t:t + blk, h * width:(h + 1) * width]
            both = jnp.concatenate([a, b], axis=0)
            g = lax.dot_general(both, both, NT, preferred_element_type=F32)
            aa, ab, bb = diag(g[:blk, :blk]), diag(g[:blk, blk:]), diag(g[blk:, blk:])
            parts.append(ab / jnp.sqrt((aa + 1.0) * (bb + 1.0)))
        return jnp.concatenate(parts, axis=1)

    odd = (iota((2 * his, toks), 0) & 1) == 1
    hi_of = iota((2 * his, toks), 0) >> 1

    def step(p):
        for c in loads(p):
            c.wait()
        for h in range(heads):
            kc = cosine(kbuf, p, h)
            vc = cosine(vbuf, p, h)
            high = bins[p, pl.ds(h, 1), :] >> shift
            left = jnp.where(hi_of == high, jnp.where(odd, vc, kc), 0.0).astype(BF16)
            res = lax.dot_general(left, lo_hot[p, h], NT, preferred_element_type=F32)
            for o in range(n):
                stage_h[p, o % 2, o // 2, pl.ds(h * per * 2, per * 2), :] = res[o * per * 2:(o + 1) * per * 2, :]

    def merge(p):
        copy_d(p).wait_recv()
        comb[:, p] = stage_h[p, core] + recv_d[p]

    def send_h(p):
        each(1, chips, lambda k: copy_h(k, p).start())

    alone = 1

    @pl.loop(0, alone)
    def _(p):
        step(p)

    pl.semaphore_wait(barrier, group - 1 + chips - 1)
    each(1, group, lambda k: copy_c(k).start())
    for p in range(alone):
        copy_d(p).start()

    @pl.loop(alone, pairs)
    def _(p):
        step(p)

        @pl.when(p == alone)
        def _():
            for q in range(alone - 1):
                merge(q)
            for q in range(alone - 1):
                send_h(q)

        merge(p - 1)
        copy_d(p).start()
        send_h(p - 1)

        @pl.when(p == alone + 2)
        def _():
            each(1, group, lambda k: copy_c(k).wait_recv())
            mine_t[...] = stage_c[spot] + jnp.sum(recv_c[1:group], axis=0)
            each(1, chips, lambda k: copy_t(k).start())

        @pl.when(p == pairs - 2)
        def _():
            each(1, chips, lambda k: copy_t(k).wait_recv())
            all_x[spot] = mine_t[...] + jnp.sum(recv_t[1:chips], axis=0)
            each(1, group, lambda k: copy_g(k, spot).start())

    merge(pairs - 1)
    send_h(pairs - 1)

    each(1, group, lambda k: copy_g(k, lax.rem(spot + group - k, group)).wait_recv())
    rows = pairs * per_c
    upper = jnp.where(iota((lanes, lanes), 0) <= iota((lanes, lanes), 1), 1.0, 0.0)
    r0, r1 = iota((rows, rows), 0), iota((rows, rows), 1)
    earlier = r1 // per_c <= r0 // per_c
    same = jnp.where(earlier & (r1 % per_c == r0 % per_c), 1.0, 0.0)
    before = jnp.where(earlier & (r1 % per_c < r0 % per_c), 1.0, 0.0)
    whole = jnp.where(earlier, 1.0, 0.0)
    row_pair = iota((rows, lanes), 0) // per_c
    goal = jnp.zeros((rows, lanes), F32)
    for p in range(pairs):
        goal = jnp.where(row_pair == p, retain[p].astype(F32), goal)

    def scan(r, carry):
        off, cnt = carry
        x = all_x[r]
        xu = exact_dot(x, upper)
        tot = jnp.broadcast_to(jnp.sum(x, axis=1, keepdims=True), (rows, lanes))
        cum = exact_dot(same, xu) + exact_dot(before, tot) + off
        cnt = cnt + jnp.where(cum < goal, 1.0, 0.0)
        return off + exact_dot(whole, tot), cnt

    zero = jnp.zeros((rows, lanes), F32)
    _, cnt = lax.fori_loop(0, group, scan, (zero, zero), unroll=group <= 8)
    for p in range(pairs):
        threshold[p] = jnp.sum(cnt[p * per_c:(p + 1) * per_c, :]).astype(jnp.int32)

    each(1, chips, lambda k: copy_h_all(k).wait_recv())
    for p in range(pairs):
        acc = comb[chip, p] + jnp.sum(recv_h[1:chips, p], axis=0)
        for h in range(heads):
            for j in range(per):
                at = (h * per + j) * 2
                out[p, h, :, j * lanes:(j + 1) * lanes] = acc[at:at + 2, :]

    each(1, group, lambda k: copy_c(k).wait_send())
    each(1, chips, lambda k: copy_t(k).wait_send())
    each(1, group, lambda k: copy_g(k, spot).wait_send())
    each(0, pairs, lambda p: copy_d(p).wait_send())
    each(1, chips, lambda k: copy_h_all(k).wait_send())


def hand_over(hist, thresh, out, threshold):
    out[...] = hist[...]
    for p in range(thresh.shape[0]):
        threshold[p] = thresh[p]


def solution(mesh):
    n, nt = mesh.shape["seq"], mesh.shape["tensor"]

    def per_device(key_states, value_states, bin_index, retain_count):
        pairs, heads, toks = bin_index.shape
        span = BINS // n
        lanes = min(128, span)
        per = span // lanes
        group, chips = 2 * nt, n // 2
        rows = pairs * BINS // lanes // group
        block = (heads * per * 2, lanes)
        vmem = pltpu.VMEM
        dma = pltpu.SemaphoreType.DMA
        hist, thresh = pl.pallas_call(
            functools.partial(kernel, n, nt),
            out_shape=(
                jax.ShapeDtypeStruct((pairs, heads, 2, span), F32),
                jax.ShapeDtypeStruct((pairs,), jnp.int32),
            ),
            in_specs=[
                pl.BlockSpec(memory_space=pl.ANY),
                pl.BlockSpec(memory_space=pl.ANY),
                pl.BlockSpec(memory_space=vmem),
                pl.BlockSpec(memory_space=pltpu.SMEM),
            ],
            out_specs=(pl.BlockSpec(memory_space=vmem), pl.BlockSpec(memory_space=pltpu.SMEM)),
            scratch_shapes=[
                vmem(key_states.shape, BF16),
                vmem(value_states.shape, BF16),
                vmem((pairs, heads, lanes, toks), BF16),
                vmem((group, rows, lanes), F32),
                vmem((group, rows, lanes), F32),
                vmem((rows, lanes), F32),
                vmem((chips, rows, lanes), F32),
                vmem((group, rows, lanes), F32),
                vmem((pairs, 2, chips) + block, F32),
                vmem((pairs, chips) + block, F32),
                vmem((chips, pairs) + block, F32),
                vmem((chips, pairs) + block, F32),
                dma((2, pairs)),
                dma((group,)), dma((group,)), dma((chips,)), dma((chips,)),
                dma((group,)), dma((group,)), dma((pairs,)), dma((pairs,)),
                dma((chips,)), dma((chips,)),
            ],
            compiler_params=pltpu.CompilerParams(collective_id=0, has_side_effects=True),
        )(key_states, value_states, bin_index, retain_count)
        specs = (pl.BlockSpec(memory_space=vmem), pl.BlockSpec(memory_space=pltpu.SMEM))
        return pl.pallas_call(
            hand_over,
            out_shape=(
                jax.ShapeDtypeStruct(hist.shape, F32),
                jax.ShapeDtypeStruct(thresh.shape, jnp.int32),
            ),
            in_specs=list(specs),
            out_specs=specs,
        )(hist, thresh)

    in_specs = (
        P(None, None, "seq", "tensor"),
        P(None, None, "seq", "tensor"),
        P(None, "tensor", "seq"),
        P(),
    )
    out_specs = (P(None, "tensor", None, "seq"), P())
    return jax.shard_map(
        per_device, mesh=mesh, in_specs=in_specs, out_specs=out_specs, check_vma=False
    )
```

profile of v0, /device:TPU:0, one launch (start us, length us, event | category | flops | bytes accessed | tf_op | source)
XLA Modules:
  0.0 24.2 jit_solution(4200438549056188672)
XLA Ops:
  0.6 22.1 %shard_map.59 = (f32[8,2,2,512]{3,2,1,0:T(2,128)}, s32[8]{0:T(128)}) custom-call(bf16[8,2,512,256]{3,2,1,0:T(8,128)(2,1)} %key_hbm.1, bf16[8,2,512,256]{3,2,1,0:T(8,128)(2,1)} %value_hbm.1, s32[8,2,512]{2,1,0:T(2,128)} %bins.1, s32[8]{0:T(128)} %retain.1), custom_call_target="tpu_custom_call" | custom-call | tf_op jit(solution)/shard_map/pallas_call | solution.py:270
  22.7 1.5 %shard_map.60 = (f32[8,2,2,512]{3,2,1,0:T(2,128)}, s32[8]{0:T(128)}) custom-call(f32[8,2,2,512]{3,2,1,0:T(2,128)} %get-tuple-element.4.hist, s32[8]{0:T(128)} %get-tuple-element.5.thresh), custom_call_target="tpu_custom_call" | custom-call | tf_op jit(solution)/shard_map/pallas_call | solution.py:304
where the time goes:
time: 24.5 us; the launch traced here: 24.2 us
  Pallas kernels  23.6 us (96%)
  between operations  0.64 us (3%)
    pallas_call x1, Pallas kernels, per_device(): pl.pallas_call(functools.partial(kernel, n, nt), out_shape=(jax.ShapeDtyp...  22.1 us
    pallas_call x1, Pallas kernels, per_device(): pl.pallas_call(hand_over, out_shape=(jax.ShapeDtypeStruct(hist.shape, F32...  1.49 us

commit v1 on v0

v1 whole, which is shorter than its diff:
```python
import functools

import jax
import jax.numpy as jnp
from jax import lax
from jax.experimental import pallas as pl
from jax.experimental.pallas import tpu as pltpu
from jax.sharding import PartitionSpec as P

BINS = 4096
LANES = 128
HALF = 64
LAG = 3
EARLY = 1
MESH = pl.DeviceIdType.MESH
NT = (((1,), (1,)), ((), ()))
F32 = jnp.float32
BF16 = jnp.bfloat16


def iota(shape, dim):
    return lax.broadcasted_iota(jnp.int32, shape, dim)


def each(lo, hi, body):
    if hi - lo <= 8:
        for k in range(lo, hi):
            body(k)
    else:

        @pl.loop(lo, hi)
        def _(k):
            body(k)


def flag(cond):
    return jnp.where(cond, jnp.ones((), BF16), jnp.zeros((), BF16))


def narrow(row):
    return row.astype(F32).astype(BF16)


def kernel(
    n, nt, key_hbm, value_hbm, bins_hbm, retain_hbm, out, thresh,
    kv, bins, retain, stage_c, recv_c, mine_t, recv_t, all_g, stage_h, recv_d, comb, recv_h,
    in_sem, bin_sem, cs, cr, ts, tr, gs, gr, ds, dr, hs, hr,
):
    pairs, heads, toks = bins.shape
    width = kv.shape[4] // heads
    lanes = stage_h.shape[4]
    his = BINS // lanes
    per = his // n
    group, chips = 2 * nt, n // 2
    own = pairs // nt
    me = lax.axis_index("seq")
    my_t = lax.axis_index("tensor")
    chip, core = me // 2, me % 2
    spot = my_t * 2 + core

    def in_plane(k):
        g = lax.rem(spot + k, group)
        return {"seq": chip * 2 + g % 2, "tensor": g // 2}

    def in_line(k):
        z = lax.rem(chip + k, chips)
        return z, {"seq": z * 2 + core}

    barrier = pltpu.get_barrier_semaphore()

    def greet(device):
        pl.semaphore_signal(barrier, inc=1, device_id=device, device_id_type=MESH)

    each(1, group, lambda k: greet(in_plane(k)))
    each(1, chips, lambda k: greet(in_line(k)[1]))

    def load(p, i):
        return pltpu.make_async_copy((key_hbm, value_hbm)[i].at[p], kv.at[p, i], in_sem.at[i, p])

    small = (
        pltpu.make_async_copy(bins_hbm, bins, bin_sem.at[0]),
        pltpu.make_async_copy(retain_hbm, retain, bin_sem.at[1]),
    )
    small[0].start()
    for p in range(EARLY):
        load(p, 0).start()
        load(p, 1).start()
    with jax.named_scope("binwait"):
        small[0].wait()
    for p in range(EARLY, pairs):
        load(p, 0).start()
        load(p, 1).start()
    small[1].start()

    shift = HALF.bit_length() - 1
    code = iota((HALF, toks), 0)
    order = narrow(jnp.where(code < HALF // 2, code * 2, code * 2 - HALF + 1))
    code = narrow(code)
    total = jnp.zeros((BINS // LANES, LANES), F32)
    for p in range(pairs):
        grid = None
        for h in range(heads):
            row = bins[p, pl.ds(h, 1), :]
            lo = flag(code == narrow(row & (HALF - 1)))
            hi = flag(order == narrow(row >> shift))
            part = lax.dot_general(hi, lo, NT, preferred_element_type=F32)
            grid = part if grid is None else grid + part
        total += jnp.concatenate([grid[:HALF // 2], grid[HALF // 2:]], axis=1)
        stage_c[p] = total

    with jax.named_scope("barrier"):
        pl.semaphore_wait(barrier, group - 1 + chips - 1)

    def copy_c(p):
        k = lax.rem(p % nt * 2 + 1 - spot + group, group)
        return k, pltpu.make_async_remote_copy(
            src_ref=stage_c.at[p], dst_ref=recv_c.at[p // nt, k], send_sem=cs, recv_sem=cr.at[p // nt],
            device_id={"seq": chip * 2 + 1, "tensor": p % nt}, device_id_type=MESH)

    def got_c(j):
        part = recv_c.at[j, pl.ds(1, group - 1)]
        return pltpu.make_async_copy(part, part, cr.at[j])

    def copy_t(j, k):
        return pltpu.make_async_remote_copy(
            src_ref=mine_t.at[j], dst_ref=recv_t.at[j, k], send_sem=ts, recv_sem=tr.at[j],
            device_id=in_line(k)[1], device_id_type=MESH)

    def got_t(j):
        part = recv_t.at[j, pl.ds(1, chips - 1)]
        return pltpu.make_async_copy(part, part, tr.at[j])

    def copy_g(k):
        return pltpu.make_async_remote_copy(
            src_ref=all_g.at[my_t], dst_ref=all_g.at[my_t], send_sem=gs, recv_sem=gr,
            device_id=in_plane(k), device_id_type=MESH)

    def got_g(m):
        part = all_g.at[pl.ds(0, m)]
        return pltpu.make_async_copy(part, part, gr)

    def copy_d(p):
        return pltpu.make_async_remote_copy(
            src_ref=stage_h.at[p, 1 - core], dst_ref=recv_d.at[p], send_sem=ds, recv_sem=dr.at[p],
            device_id={"seq": chip * 2 + 1 - core}, device_id_type=MESH)

    def copy_h(k, p):
        z, device = in_line(k)
        return pltpu.make_async_remote_copy(
            src_ref=comb.at[z, p], dst_ref=recv_h.at[k, p], send_sem=hs, recv_sem=hr,
            device_id=device, device_id_type=MESH)

    def got_h():
        part = recv_h.at[pl.ds(1, chips - 1)]
        return pltpu.make_async_copy(part, part, hr)

    for p in range(pairs):
        k, copy = copy_c(p)
        pl.when(k > 0)(copy.start)

    blk = LANES
    eye = flag(iota((width, width), 0) == iota((width, width), 1))

    def cosine(p, i, h):
        parts = []
        for t in range(0, toks, blk):
            a = kv[p, i, 0, t:t + blk, h * width:(h + 1) * width]
            b = kv[p, i, 1, t:t + blk, h * width:(h + 1) * width]
            if t // blk in (0, 1, 2, 3):
                a, b = a.T.astype(F32), b.T.astype(F32)
            else:
                both = jnp.concatenate([a, b], axis=0)
                turned = lax.dot_general(eye, both, NT, preferred_element_type=F32)
                a, b = turned[:, :blk], turned[:, blk:]
            ab, aa, bb = (jnp.sum(x, axis=0, keepdims=True) for x in (a * b, a * a, b * b))
            parts.append(ab * lax.rsqrt((aa + 1.0) * (bb + 1.0)))
        return jnp.concatenate(parts, axis=1)

    cut = lanes.bit_length() - 1
    odd = (iota((2 * his, toks), 0) & 1) == 1
    hi_of = narrow(iota((2 * his, toks), 0) >> 1)
    lo_of = narrow(iota((lanes, toks), 0))

    def step(p):
        with jax.named_scope("loadwait"):
            load(p, 0).wait()
            load(p, 1).wait()
        for h in range(heads):
            kc = cosine(p, 0, h)
            vc = cosine(p, 1, h)
            row = bins[p, pl.ds(h, 1), :]
            both = jnp.where(odd, vc, kc).astype(BF16)
            left = jnp.where(hi_of == narrow(row >> cut), both, jnp.zeros_like(both))
            right = flag(lo_of == narrow(row & (lanes - 1)))
            res = lax.dot_general(left, right, NT, preferred_element_type=F32)
            for o in range(n):
                stage_h[p, o % 2, o // 2, pl.ds(h * per * 2, per * 2), :] = res[o * per * 2:(o + 1) * per * 2, :]

    def merge(p):
        with jax.named_scope("waitd"):
            copy_d(p).wait_recv()
        comb[:, p] = stage_h[p, core] + recv_d[p]
        each(1, chips, lambda k: copy_h(k, p).start())

    @pl.loop(0, pairs)
    def _(p):
        step(p)
        copy_d(p).start()

        @pl.when(p >= LAG)
        def _():
            merge(p - LAG)

    for p in range(pairs - LAG, pairs - 1):
        merge(p)

    @pl.when(core == 1)
    def _():
        for j in range(own):
            with jax.named_scope("waitc"):
                got_c(j).wait()
            mine_t[j] = stage_c[j * nt + my_t] + jnp.sum(recv_c[j, 1:group], axis=0)
            each(1, chips, lambda k: copy_t(j, k).start())

    merge(pairs - 1)

    @pl.when(core == 1)
    def _():
        rows = BINS // LANES
        small[1].wait()
        xs = []
        for j in range(own):
            with jax.named_scope("waitt"):
                got_t(j).wait()
            xs.append(mine_t[j] + jnp.sum(recv_t[j, 1:chips], axis=0))
        x = jnp.concatenate(xs, axis=0)
        top = jnp.floor(x * (1.0 / 65536.0))
        x = x - top * 65536.0
        mid = jnp.floor(x * (1.0 / 256.0))
        low = x - mid * 256.0
        digits = [v.astype(BF16) for v in (low, mid, top)]
        size = own * rows
        r0, r1 = iota((size, size), 0), iota((size, size), 1)
        upper = flag(iota((LANES, LANES), 0) <= iota((LANES, LANES), 1))
        before = flag((r0 // rows == r1 // rows) & (r1 < r0))

        def value(parts):
            return parts[0] + parts[1] * 256.0 + parts[2] * 65536.0

        within = value([jnp.dot(v, upper, preferred_element_type=F32) for v in digits])
        ahead = value([jnp.dot(before, v, preferred_element_type=F32) for v in digits])
        cum = within + jnp.sum(ahead, axis=1, keepdims=True)
        for j in range(own):
            goal = retain[j * nt + my_t].astype(F32)
            less = jnp.where(cum[j * rows:(j + 1) * rows] < goal, 1.0, 0.0)
            all_g[my_t, j] = jnp.sum(less, axis=0, keepdims=True)
        each(1, group, lambda k: copy_g(k).start())
        with jax.named_scope("waitg"):
            got_g(nt - 1).wait()

    @pl.when(core == 0)
    def _():
        small[1].wait()
        with jax.named_scope("waitg"):
            got_g(nt).wait()

    counts = jnp.concatenate([all_g[p % nt, p // nt] for p in range(pairs)], axis=0)
    if pairs < LANES:
        counts = jnp.concatenate([counts, jnp.zeros((LANES - pairs, LANES), F32)], axis=0)
    ones = jnp.ones((8, LANES), BF16)
    found = lax.dot_general(ones, counts.astype(BF16), NT, preferred_element_type=F32)
    thresh[...] = found.astype(jnp.int32)

    with jax.named_scope("waith"):
        got_h().wait()
    for p in range(pairs):
        acc = comb[chip, p] + jnp.sum(recv_h[1:chips, p], axis=0)
        for h in range(heads):
            for j in range(per):
                at = (h * per + j) * 2
                out[p, h, :, j * lanes:(j + 1) * lanes] = acc[at:at + 2, :]

    for p in range(pairs):
        k, copy = copy_c(p)
        pl.when(k > 0)(copy.wait_send)

    @pl.when(core == 1)
    def _():
        for j in range(own):
            each(1, chips, lambda k: copy_t(j, k).wait_send())
        each(1, group, lambda k: copy_g(k).wait_send())

    each(0, pairs, lambda p: copy_d(p).wait_send())
    whole = comb.at[pl.ds(0, chips - 1)]
    pltpu.make_async_copy(whole, whole, hs).wait()


def hand_over(hist, thresh, out, threshold):
    out[...] = hist[...]
    threshold[...] = thresh[0, :threshold.shape[0]]


def solution(mesh):
    n, nt = mesh.shape["seq"], mesh.shape["tensor"]

    def per_device(key_states, value_states, bin_index, retain_count):
        pairs, heads, toks = bin_index.shape
        span = BINS // n
        lanes = min(LANES, span)
        per = span // lanes
        group, chips = 2 * nt, n // 2
        own = pairs // nt
        rows = BINS // LANES
        block = (heads * per * 2, lanes)
        vmem = pltpu.VMEM
        dma = pltpu.SemaphoreType.DMA
        args = [
            pltpu.with_memory_space_constraint(x, pltpu.HBM)
            for x in (key_states, value_states, bin_index, retain_count)
        ]
        hist, thresh = pl.pallas_call(
            functools.partial(kernel, n, nt),
            out_shape=(
                jax.ShapeDtypeStruct((pairs, heads, 2, span), F32),
                jax.ShapeDtypeStruct((8, LANES), jnp.int32),
            ),
            in_specs=[pl.BlockSpec(memory_space=pltpu.HBM)] * 4,
            out_specs=(pl.BlockSpec(memory_space=vmem), pl.BlockSpec(memory_space=vmem)),
            scratch_shapes=[
                vmem((pairs, 2) + key_states.shape[1:], BF16),
                vmem(bin_index.shape, jnp.int32),
                pltpu.SMEM(retain_count.shape, jnp.int32),
                vmem((pairs, rows, LANES), F32),
                vmem((own, group, rows, LANES), F32),
                vmem((own, rows, LANES), F32),
                vmem((own, chips, rows, LANES), F32),
                vmem((nt, own, 1, LANES), F32),
                vmem((pairs, 2, chips) + block, F32),
                vmem((pairs, chips) + block, F32),
                vmem((chips, pairs) + block, F32),
                vmem((chips, pairs) + block, F32),
                dma((2, pairs)), dma((2,)),
                dma, dma((own,)), dma, dma((own,)),
                dma, dma, dma, dma((pairs,)),
                dma, dma,
            ],
            compiler_params=pltpu.CompilerParams(
                collective_id=0, has_side_effects=True, vmem_limit_bytes=32 * 2**20
            ),
        )(*args)
        return pl.pallas_call(
            hand_over,
            out_shape=(
                jax.ShapeDtypeStruct(hist.shape, F32),
                jax.ShapeDtypeStruct(retain_count.shape, jnp.int32),
            ),
            in_specs=[pl.BlockSpec(memory_space=vmem)] * 2,
            out_specs=(pl.BlockSpec(memory_space=vmem), pl.BlockSpec(memory_space=vmem)),
            compiler_params=pltpu.CompilerParams(vmem_limit_bytes=4 * 2**20),
        )(hist, thresh)

    in_specs = (
        P(None, None, "seq", "tensor"),
        P(None, None, "seq", "tensor"),
        P(None, "tensor", "seq"),
        P(),
    )
    out_specs = (P(None, "tensor", None, "seq"), P())
    return jax.shard_map(
        per_device, mesh=mesh, in_specs=in_specs, out_specs=out_specs, check_vma=False
    )
```

time: 24.5 us -> 21.4 us (0.87)
  Pallas kernels: 23.6 us -> 20.6 us
    pallas_call x1, Pallas kernels: 22.1 us -> 19.9 us  [per_device(): pl.pallas_call(functools.partial(kernel, n, nt), out_shape=(jax.ShapeDtyp...]
    pallas_call x1, Pallas kernels: 1.49 us -> 0.64 us  [per_device(): pl.pallas_call(hand_over, out_shape=(jax.ShapeDtypeStruct(hist.shape, F32...]
where the time goes in v1:
time: 21.4 us; the launch traced here: 21.2 us
  Pallas kernels  20.6 us (96%)
  between operations  0.64 us (3%)
    pallas_call x1, Pallas kernels, per_device(): pl.pallas_call(functools.partial(kernel, n, nt), out_shape=(jax.ShapeDtyp...  19.9 us
    pallas_call x1, Pallas kernels, per_device(): pl.pallas_call(hand_over, out_shape=(jax.ShapeDtypeStruct(hist.shape, F32...  0.64 us

profile of v1, /device:TPU:0, one launch (start us, length us, event | category | flops | bytes accessed | tf_op | source)
XLA Modules:
  0.0 21.2 jit_solution(14875305955289156705)
XLA Ops:
  0.6 19.9 %shard_map.59 = (f32[8,2,2,512]{3,2,1,0:T(2,128)S(1)}, s32[8,128]{1,0:T(8,128)S(1)}) custom-call(bf16[8,2,512,256]{3,2,1,0:T(8,128)(2,1)} %key_hbm.1, bf16[8,2,512,256]{3,2,1,0:T(8,128)(2,1)} %value_hbm.1, s32[8,2,512]{2,1,0:T(2,128)} %bins_hbm.1, s32[8]{0:T(128)} %retain_hbm.1), custom_call_target="tpu_custom_call" | custom-call | tf_op jit(solution)/shard_map/pallas_call | solution.py:321
  20.6 0.6 %shard_map.60 = (f32[8,2,2,512]{3,2,1,0:T(2,128)}, s32[8]{0:T(128)}) custom-call(f32[8,2,2,512]{3,2,1,0:T(2,128)S(1)} %get-tuple-element.4.hist, s32[8,128]{1,0:T(8,128)S(1)} %get-tuple-element.5.thresh), custom_call_target="tpu_custom_call" | custom-call | tf_op jit(solution)/shard_map/pallas_call | solution.py:351

commit v2 on v1

--- a/solution.py
+++ b/solution.py
@@ -10,8 +10,9 @@
 BINS = 4096
 LANES = 128
 HALF = 64
-LAG = 3
+LAG = 2
 EARLY = 1
+TURN = 5
 MESH = pl.DeviceIdType.MESH
 NT = (((1,), (1,)), ((), ()))
 F32 = jnp.float32
@@ -211,18 +212,16 @@
         def _():
             merge(p - LAG)
 
-    for p in range(pairs - LAG, pairs - 1):
+        @pl.when((p == pairs - TURN) & (core == 1))
+        def _():
+            for j in range(own):
+                with jax.named_scope("waitc"):
+                    got_c(j).wait()
+                mine_t[j] = stage_c[j * nt + my_t] + jnp.sum(recv_c[j, 1:group], axis=0)
+                each(1, chips, lambda k: copy_t(j, k).start())
+
+    for p in range(pairs - LAG, pairs):
         merge(p)
-
-    @pl.when(core == 1)
-    def _():
-        for j in range(own):
-            with jax.named_scope("waitc"):
-                got_c(j).wait()
-            mine_t[j] = stage_c[j * nt + my_t] + jnp.sum(recv_c[j, 1:group], axis=0)
-            each(1, chips, lambda k: copy_t(j, k).start())
-
-    merge(pairs - 1)
 
     @pl.when(core == 1)
     def _():

time: 21.4 us -> 17.9 us (0.84)
  Pallas kernels: 20.6 us -> 17.1 us
    pallas_call x1, Pallas kernels: 19.9 us -> 16.5 us  [per_device(): pl.pallas_call(functools.partial(kernel, n, nt), out_shape=(jax.ShapeDtyp...]
where the time goes in v2:
time: 17.9 us; the launch traced here: 17.8 us
  Pallas kernels  17.1 us (96%)
  between operations  0.64 us (4%)
    pallas_call x1, Pallas kernels, per_device(): pl.pallas_call(functools.partial(kernel, n, nt), out_shape=(jax.ShapeDtyp...  16.5 us
    pallas_call x1, Pallas kernels, per_device(): pl.pallas_call(hand_over, out_shape=(jax.ShapeDtypeStruct(hist.shape, F32...  0.64 us

profile of v2, /device:TPU:0, one launch (start us, length us, event | category | flops | bytes accessed | tf_op | source)
XLA Modules:
  0.0 17.8 jit_solution(11597962660443395296)
XLA Ops:
  0.6 16.5 %shard_map.59 = (f32[8,2,2,512]{3,2,1,0:T(2,128)S(1)}, s32[8,128]{1,0:T(8,128)S(1)}) custom-call(bf16[8,2,512,256]{3,2,1,0:T(8,128)(2,1)} %key_hbm.1, bf16[8,2,512,256]{3,2,1,0:T(8,128)(2,1)} %value_hbm.1, s32[8,2,512]{2,1,0:T(2,128)} %bins_hbm.1, s32[8]{0:T(128)} %retain_hbm.1), custom_call_target="tpu_custom_call" | custom-call | tf_op jit(solution)/shard_map/pallas_call | solution.py:320
  17.1 0.6 %shard_map.60 = (f32[8,2,2,512]{3,2,1,0:T(2,128)}, s32[8]{0:T(128)}) custom-call(f32[8,2,2,512]{3,2,1,0:T(2,128)S(1)} %get-tuple-element.4.hist, s32[8,128]{1,0:T(8,128)S(1)} %get-tuple-element.5.thresh), custom_call_target="tpu_custom_call" | custom-call | tf_op jit(solution)/shard_map/pallas_call | solution.py:350

commit v3 on v2

--- a/solution.py
+++ b/solution.py
@@ -13,6 +13,7 @@
 LAG = 2
 EARLY = 1
 TURN = 5
+RELAY = 4
 MESH = pl.DeviceIdType.MESH
 NT = (((1,), (1,)), ((), ()))
 F32 = jnp.float32
@@ -44,8 +45,8 @@
 
 def kernel(
     n, nt, key_hbm, value_hbm, bins_hbm, retain_hbm, out, thresh,
-    kv, bins, retain, stage_c, recv_c, mine_t, recv_t, all_g, stage_h, recv_d, comb, recv_h,
-    in_sem, bin_sem, cs, cr, ts, tr, gs, gr, ds, dr, hs, hr,
+    kv, bins, retain, stage_c, recv_c, mine_t, recv_t, all_g, stage_h, recv_d, comb, recv_h, recv_r,
+    in_sem, bin_sem, cs, cr, ts, tr, gs, gr, ds, dr, hs, hr, rr,
 ):
     pairs, heads, toks = bins.shape
     width = kv.shape[4] // heads
@@ -67,6 +68,22 @@
         z = lax.rem(chip + k, chips)
         return z, {"seq": z * 2 + core}
 
+    relay = recv_r.shape[0] if chips == 4 else 0
+
+    def mirror(z, r):
+        return jnp.where(r < chips // 2, z, chips - 1 - z)
+
+    spoke = mirror(chip, chip)
+    inner = spoke == 1
+
+    def nth(i):
+        return lax.rem(i + jnp.where(inner, relay, 0), pairs) if relay else i
+
+    def slot(z):
+        if relay:
+            return jnp.maximum(mirror(chip, z) - 1, 0)
+        return lax.rem(z - chip + chips, chips) - 1
+
     barrier = pltpu.get_barrier_semaphore()
 
     def greet(device):
@@ -84,13 +101,13 @@
     )
     small[0].start()
     for p in range(EARLY):
-        load(p, 0).start()
-        load(p, 1).start()
+        load(nth(p), 0).start()
+        load(nth(p), 1).start()
     with jax.named_scope("binwait"):
         small[0].wait()
     for p in range(EARLY, pairs):
-        load(p, 0).start()
-        load(p, 1).start()
+        load(nth(p), 0).start()
+        load(nth(p), 1).start()
     small[1].start()
 
     shift = HALF.bit_length() - 1
@@ -145,15 +162,22 @@
             src_ref=stage_h.at[p, 1 - core], dst_ref=recv_d.at[p], send_sem=ds, recv_sem=dr.at[p],
             device_id={"seq": chip * 2 + 1 - core}, device_id_type=MESH)
 
-    def copy_h(k, p):
-        z, device = in_line(k)
+    def copy_h(z, p):
+        to = slot(z)
         return pltpu.make_async_remote_copy(
-            src_ref=comb.at[z, p], dst_ref=recv_h.at[k, p], send_sem=hs, recv_sem=hr,
-            device_id=device, device_id_type=MESH)
-
-    def got_h():
-        part = recv_h.at[pl.ds(1, chips - 1)]
-        return pltpu.make_async_copy(part, part, hr)
+            src_ref=comb.at[z, p], dst_ref=recv_h.at[to, p], send_sem=hs, recv_sem=hr.at[to // 2 if relay else 0],
+            device_id={"seq": z * 2 + core}, device_id_type=MESH)
+
+    def copy_r(i, p):
+        return pltpu.make_async_remote_copy(
+            src_ref=comb.at[mirror(2 + i, chip), p], dst_ref=recv_r.at[p, i], send_sem=hs, recv_sem=rr.at[p],
+            device_id={"seq": mirror(1, chip) * 2 + core}, device_id_type=MESH)
+
+    def wait_h():
+        if not relay:
+            return pltpu.make_async_copy(recv_h, recv_h, hr.at[0]).wait()
+        for i, part in enumerate((recv_h.at[pl.ds(0, 2)], recv_h.at[2, pl.ds(relay, pairs - relay)])):
+            pltpu.make_async_copy(part, part, hr.at[i]).wait()
 
     for p in range(pairs):
         k, copy = copy_c(p)
@@ -197,22 +221,43 @@
             for o in range(n):
                 stage_h[p, o % 2, o // 2, pl.ds(h * per * 2, per * 2), :] = res[o * per * 2:(o + 1) * per * 2, :]
 
-    def merge(p):
+    def merge(i):
+        p = nth(i)
         with jax.named_scope("waitd"):
             copy_d(p).wait_recv()
         comb[:, p] = stage_h[p, core] + recv_d[p]
-        each(1, chips, lambda k: copy_h(k, p).start())
+        if not relay:
+            return each(1, chips, lambda k: copy_h(in_line(k)[0], p).start())
+
+        @pl.when((p < relay) & jnp.logical_not(inner))
+        def _():
+            copy_r(0, p).start()
+            copy_r(1, p).start()
+            copy_h(mirror(1, chip), p).start()
+
+        @pl.when((p < relay) & inner)
+        def _():
+            got = recv_r.at[p]
+            with jax.named_scope("waitr"):
+                pltpu.make_async_copy(got, got, rr.at[p]).wait()
+            for i in range(2):
+                comb[mirror(2 + i, chip), p] += recv_r[p, i]
+
+        @pl.when((p >= relay) | inner)
+        def _():
+            each(1, chips, lambda k: copy_h(in_line(k)[0], p).start())
 
     @pl.loop(0, pairs)
-    def _(p):
+    def _(i):
+        p = nth(i)
         step(p)
         copy_d(p).start()
 
-        @pl.when(p >= LAG)
+        @pl.when(i >= LAG)
         def _():
-            merge(p - LAG)
-
-        @pl.when((p == pairs - TURN) & (core == 1))
+            merge(i - LAG)
+
+        @pl.when((i == pairs - TURN) & (core == 1))
         def _():
             for j in range(own):
                 with jax.named_scope("waitc"):
@@ -271,9 +316,9 @@
     thresh[...] = found.astype(jnp.int32)
 
     with jax.named_scope("waith"):
-        got_h().wait()
+        wait_h()
     for p in range(pairs):
-        acc = comb[chip, p] + jnp.sum(recv_h[1:chips, p], axis=0)
+        acc = comb[chip, p] + jnp.sum(recv_h[:2 if p < relay else chips - 1, p], axis=0)
         for h in range(heads):
             for j in range(per):
                 at = (h * per + j) * 2
@@ -337,11 +382,12 @@
                 vmem((pairs, 2, chips) + block, F32),
                 vmem((pairs, chips) + block, F32),
                 vmem((chips, pairs) + block, F32),
-                vmem((chips, pairs) + block, F32),
+                vmem((chips - 1, pairs) + block, F32),
+                vmem((RELAY, 2) + block, F32),
                 dma((2, pairs)), dma((2,)),
                 dma, dma((own,)), dma, dma((own,)),
                 dma, dma, dma, dma((pairs,)),
-                dma, dma,
+                dma, dma((2,)), dma((RELAY,)),
             ],
             compiler_params=pltpu.CompilerParams(
                 collective_id=0, has_side_effects=True, vmem_limit_bytes=32 * 2**20

time: 17.9 us -> 17.6 us (0.983)
  Pallas kernels: 17.1 us -> 16.8 us
    pallas_call x1, Pallas kernels: 16.5 us -> 16.1 us  [per_device(): pl.pallas_call(functools.partial(kernel, n, nt), out_shape=(jax.ShapeDtyp...]
where the time goes in v3:
time: 17.6 us; the launch traced here: 17.4 us
  Pallas kernels  16.8 us (95%)
  between operations  0.64 us (4%)
    pallas_call x1, Pallas kernels, per_device(): pl.pallas_call(functools.partial(kernel, n, nt), out_shape=(jax.ShapeDtyp...  16.1 us
    pallas_call x1, Pallas kernels, per_device(): pl.pallas_call(hand_over, out_shape=(jax.ShapeDtypeStruct(hist.shape, F32...  0.64 us

profile of v3, /device:TPU:0, one launch (start us, length us, event | category | flops | bytes accessed | tf_op | source)
XLA Modules:
  0.0 17.4 jit_solution(8947445144750774118)
XLA Ops:
  0.6 16.1 %shard_map.59 = (f32[8,2,2,512]{3,2,1,0:T(2,128)S(1)}, s32[8,128]{1,0:T(8,128)S(1)}) custom-call(bf16[8,2,512,256]{3,2,1,0:T(8,128)(2,1)} %key_hbm.1, bf16[8,2,512,256]{3,2,1,0:T(8,128)(2,1)} %value_hbm.1, s32[8,2,512]{2,1,0:T(2,128)} %bins_hbm.1, s32[8]{0:T(128)} %retain_hbm.1), custom_call_target="tpu_custom_call" | custom-call | tf_op jit(solution)/shard_map/pallas_call | solution.py:365
  16.8 0.6 %shard_map.60 = (f32[8,2,2,512]{3,2,1,0:T(2,128)}, s32[8]{0:T(128)}) custom-call(f32[8,2,2,512]{3,2,1,0:T(2,128)S(1)} %get-tuple-element.4.hist, s32[8,128]{1,0:T(8,128)S(1)} %get-tuple-element.5.thresh), custom_call_target="tpu_custom_call" | custom-call | tf_op jit(solution)/shard_map/pallas_call | solution.py:396

commit v4 on v3

--- a/solution.py
+++ b/solution.py
@@ -12,8 +12,9 @@
 HALF = 64
 LAG = 2
 EARLY = 1
-TURN = 5
+TURN = 4
 RELAY = 4
+ALONE = 1
 MESH = pl.DeviceIdType.MESH
 NT = (((1,), (1,)), ((), ()))
 F32 = jnp.float32
@@ -93,7 +94,7 @@
     each(1, chips, lambda k: greet(in_line(k)[1]))
 
     def load(p, i):
-        return pltpu.make_async_copy((key_hbm, value_hbm)[i].at[p], kv.at[p, i], in_sem.at[i, p])
+        return pltpu.make_async_copy((key_hbm, value_hbm)[i].at[p], kv.at[p, i], in_sem.at[p])
 
     small = (
         pltpu.make_async_copy(bins_hbm, bins, bin_sem.at[0]),
@@ -126,9 +127,6 @@
         total += jnp.concatenate([grid[:HALF // 2], grid[HALF // 2:]], axis=1)
         stage_c[p] = total
 
-    with jax.named_scope("barrier"):
-        pl.semaphore_wait(barrier, group - 1 + chips - 1)
-
     def copy_c(p):
         k = lax.rem(p % nt * 2 + 1 - spot + group, group)
         return k, pltpu.make_async_remote_copy(
@@ -178,10 +176,6 @@
             return pltpu.make_async_copy(recv_h, recv_h, hr.at[0]).wait()
         for i, part in enumerate((recv_h.at[pl.ds(0, 2)], recv_h.at[2, pl.ds(relay, pairs - relay)])):
             pltpu.make_async_copy(part, part, hr.at[i]).wait()
-
-    for p in range(pairs):
-        k, copy = copy_c(p)
-        pl.when(k > 0)(copy.start)
 
     blk = LANES
     eye = flag(iota((width, width), 0) == iota((width, width), 1))
@@ -208,8 +202,7 @@
 
     def step(p):
         with jax.named_scope("loadwait"):
-            load(p, 0).wait()
-            load(p, 1).wait()
+            pltpu.make_async_copy(kv.at[p], kv.at[p], in_sem.at[p]).wait()
         for h in range(heads):
             kc = cosine(p, 0, h)
             vc = cosine(p, 1, h)
@@ -247,7 +240,21 @@
         def _():
             each(1, chips, lambda k: copy_h(in_line(k)[0], p).start())
 
-    @pl.loop(0, pairs)
+    @pl.loop(0, ALONE)
+    def _(i):
+        step(nth(i))
+
+    with jax.named_scope("barrier"):
+        pl.semaphore_wait(barrier, group - 1 + chips - 1)
+
+    for p in range(pairs):
+        k, copy = copy_c(p)
+        pl.when(k > 0)(copy.start)
+
+    for i in range(ALONE):
+        copy_d(nth(i)).start()
+
+    @pl.loop(ALONE, pairs)
     def _(i):
         p = nth(i)
         step(p)
@@ -299,21 +306,6 @@
             less = jnp.where(cum[j * rows:(j + 1) * rows] < goal, 1.0, 0.0)
             all_g[my_t, j] = jnp.sum(less, axis=0, keepdims=True)
         each(1, group, lambda k: copy_g(k).start())
-        with jax.named_scope("waitg"):
-            got_g(nt - 1).wait()
-
-    @pl.when(core == 0)
-    def _():
-        small[1].wait()
-        with jax.named_scope("waitg"):
-            got_g(nt).wait()
-
-    counts = jnp.concatenate([all_g[p % nt, p // nt] for p in range(pairs)], axis=0)
-    if pairs < LANES:
-        counts = jnp.concatenate([counts, jnp.zeros((LANES - pairs, LANES), F32)], axis=0)
-    ones = jnp.ones((8, LANES), BF16)
-    found = lax.dot_general(ones, counts.astype(BF16), NT, preferred_element_type=F32)
-    thresh[...] = found.astype(jnp.int32)
 
     with jax.named_scope("waith"):
         wait_h()
@@ -323,6 +315,24 @@
             for j in range(per):
                 at = (h * per + j) * 2
                 out[p, h, :, j * lanes:(j + 1) * lanes] = acc[at:at + 2, :]
+
+    @pl.when(core == 1)
+    def _():
+        with jax.named_scope("waitg"):
+            got_g(nt - 1).wait()
+
+    @pl.when(core == 0)
+    def _():
+        small[1].wait()
+        with jax.named_scope("waitg"):
+            got_g(nt).wait()
+
+    counts = jnp.concatenate([all_g[p % nt, p // nt] for p in range(pairs)], axis=0)
+    if pairs < LANES:
+        counts = jnp.concatenate([counts, jnp.zeros((LANES - pairs, LANES), F32)], axis=0)
+    ones = jnp.ones((8, LANES), BF16)
+    found = lax.dot_general(ones, counts.astype(BF16), NT, preferred_element_type=F32)
+    thresh[...] = found.astype(jnp.int32)
 
     for p in range(pairs):
         k, copy = copy_c(p)
@@ -384,7 +394,7 @@
                 vmem((chips, pairs) + block, F32),
                 vmem((chips - 1, pairs) + block, F32),
                 vmem((RELAY, 2) + block, F32),
-                dma((2, pairs)), dma((2,)),
+                dma((pairs,)), dma((2,)),
                 dma, dma((own,)), dma, dma((own,)),
                 dma, dma, dma, dma((pairs,)),
                 dma, dma((2,)), dma((RELAY,)),

time: 17.6 us -> 17.6 us (level)
  no operation moved by 1% of the time
where the time goes in v4:
time: 17.6 us; the launch traced here: 17.5 us
  Pallas kernels  16.8 us (95%)
  between operations  0.64 us (4%)
    pallas_call x1, Pallas kernels, per_device(): pl.pallas_call(functools.partial(kernel, n, nt), out_shape=(jax.ShapeDtyp...  16.2 us
    pallas_call x1, Pallas kernels, per_device(): pl.pallas_call(hand_over, out_shape=(jax.ShapeDtypeStruct(hist.shape, F32...  0.64 us

profile of v4, /device:TPU:0, one launch (start us, length us, event | category | flops | bytes accessed | tf_op | source)
XLA Modules:
  0.0 17.5 jit_solution(16951374324222783306)
XLA Ops:
  0.6 16.2 %shard_map.59 = (f32[8,2,2,512]{3,2,1,0:T(2,128)S(1)}, s32[8,128]{1,0:T(8,128)S(1)}) custom-call(bf16[8,2,512,256]{3,2,1,0:T(8,128)(2,1)} %key_hbm.1, bf16[8,2,512,256]{3,2,1,0:T(8,128)(2,1)} %value_hbm.1, s32[8,2,512]{2,1,0:T(2,128)} %bins_hbm.1, s32[8]{0:T(128)} %retain_hbm.1), custom_call_target="tpu_custom_call" | custom-call | tf_op jit(solution)/shard_map/pallas_call | solution.py:375
  16.8 0.6 %shard_map.60 = (f32[8,2,2,512]{3,2,1,0:T(2,128)}, s32[8]{0:T(128)}) custom-call(f32[8,2,2,512]{3,2,1,0:T(2,128)S(1)} %get-tuple-element.4.hist, s32[8,128]{1,0:T(8,128)S(1)} %get-tuple-element.5.thresh), custom_call_target="tpu_custom_call" | custom-call | tf_op jit(solution)/shard_map/pallas_call | solution.py:406
